TPU v7x, 32 devices: a whole 2x2x4 slice. The times are simulated.
32 devices in a mesh: wa: 4 (over z), bl: 8 (over y, x, core).
Axes of the slice: x: 2, y: 2, z: 4, core: 2. Of those that a mesh axis runs over, the one named last changes fastest.
Arguments:
- visibilities: float32 [4, 16, 2, 128], P('wa', 'bl'), may hold values from -6 to 6
- weights: float32 [4, 16, 128], P('wa', 'bl'), may hold values from 0.25 to 4
- cell_index: int32 [4, 16, 128], P('wa', 'bl'), may hold values from 0 to 1048575
- kernel_index: int32 [4, 16, 128], P('wa', 'bl'), may hold values from 0 to 255
- layer_index: int32 [4, 16, 128], P('wa', 'bl'), may hold values from 0 to 1
- tile_counts: int32 [4, 16], P('wa', 'bl'), may hold values from 1 to 128
- kernel_table: float32 [16, 8], replicated, may hold values from 0.05 to 0.3
- layer_depth: float32 [8], P('wa'), may hold values from -150 to 150
Outputs:
- image: float32 [1024, 1024], P('wa', 'bl')
All inputs are finite; a program needn't handle non-finite values.
Results may differ from a plain program's by a relative error of at most 0.0003.
Values sent between devices are 32-bit elements; how exact they have to be, the bound alone decides.
A program may use at most 128 MiB of HBM per device.

v0:
```python
import functools
import math

import jax
import jax.numpy as jnp
from jax import lax
from jax.experimental import pallas as pl
from jax.experimental.pallas import tpu as pltpu
from jax.sharding import PartitionSpec as P

GRID = 1024
SUPPORT = 8
OVERSAMPLE = 16
LANES = 128
FINE = 32
XBLOCK = 128

field_of_view = 0.6
MESH = pl.DeviceIdType.MESH

TWO_PI = 2.0 * math.pi
SIN_TERMS = [(-1) ** k * TWO_PI ** (2 * k + 1) / math.factorial(2 * k + 1) for k in range(9)]
COS_TERMS = [(-1) ** k * TWO_PI ** (2 * k) / math.factorial(2 * k) for k in range(10)]


def horner(square, terms):
    value = jnp.full_like(square, terms[-1])
    for term in terms[-2::-1]:
        value = value * square + term
    return value


def turn_cos_sin(turns):
    part = turns - jnp.round(turns)
    square = part * part
    return horner(square, COS_TERMS), part * horner(square, SIN_TERMS)


def split(value):
    high = value.astype(jnp.bfloat16)
    return high, (value - high.astype(jnp.float32)).astype(jnp.bfloat16)


def dot_nt(a, b):
    return lax.dot_general(
        a, b, (((1,), (1,)), ((), ())), preferred_element_type=jnp.float32
    )


def greet(axis, me, count):
    barrier = pltpu.get_barrier_semaphore()
    for step in range(1, count):
        pl.semaphore_signal(
            barrier, inc=1, device_id={axis: lax.rem(me + step, count)}, device_id_type=MESH
        )
    pl.semaphore_wait(barrier, count - 1)


def gather_kernel(count, own_ref, all_ref, send_sem, recv_sem):
    me = lax.axis_index("bl")
    greet("bl", me, count)
    copies = []
    for step in range(1, count):
        copy = pltpu.make_async_remote_copy(
            src_ref=own_ref,
            dst_ref=all_ref.at[me],
            send_sem=send_sem.at[step - 1],
            recv_sem=recv_sem.at[step - 1],
            device_id={"bl": lax.rem(me + step, count)},
            device_id_type=MESH,
        )
        copy.start()
        copies.append(copy)
    all_ref[me] = own_ref[...]
    for copy in copies:
        copy.wait()


def factor_table(first, rows, table, special):
    pixel = (first + lax.broadcasted_iota(jnp.int32, (rows, LANES), 0)).astype(jnp.float32)
    offset_lane = lax.broadcasted_iota(jnp.int32, (rows, LANES), 1)
    offset = (offset_lane % SUPPORT - SUPPORT // 2).astype(jnp.float32)
    cos_part, sin_part = turn_cos_sin(pixel * offset * (1.0 / GRID))
    if special:
        row = lax.broadcasted_iota(jnp.int32, (rows, LANES), 0)
        parity = 1.0 - 2.0 * (offset_lane % 2).astype(jnp.float32)
        sin_part = jnp.where(row == 0, parity, sin_part)
    table_high, table_low = split(table)

    def product(part):
        high, low = split(part)
        return dot_nt(high, table_high) + dot_nt(high, table_low) + dot_nt(low, table_high)

    return product(cos_part), product(sin_part)


def compute_kernel(
    layer_dev,
    pixels,
    blocks,
    depth_ref,
    table_ref,
    slots_ref,
    out_ref,
    table_pad,
    u_re,
    u_im,
    fine_re,
    fine_im,
    coarse_re,
    coarse_im,
    w_high,
    w_low,
    lhs_high,
    lhs_low,
    neg,
):
    half = GRID // 2
    tiles = slots_ref.shape[0]
    chunk_rows = GRID // blocks
    first_pixel = lax.axis_index("bl") * pixels
    table_pad[...] = jnp.zeros_like(table_pad)
    table_pad[0:OVERSAMPLE, 0:SUPPORT] = table_ref[...]
    table = table_pad[...]
    u_re[...], u_im[...] = factor_table(0, half, table, True)
    v_re, v_im = factor_table(first_pixel, pixels, table, False)
    fine_x = lax.broadcasted_iota(jnp.int32, (FINE, LANES), 0).astype(jnp.float32)
    coarse_x = (lax.broadcasted_iota(jnp.int32, (half // FINE, LANES), 0) * FINE).astype(
        jnp.float32
    )
    pixel_y = (
        first_pixel + lax.broadcasted_iota(jnp.int32, (pixels // FINE, LANES), 0) * FINE
    ).astype(jnp.float32)

    def prepare(tile, square):
        lanes = pl.ds(pl.multiple_of(tile * LANES, LANES), LANES)
        params = slots_ref[tile]
        vis_real, vis_imag, weight = params[0:1], params[1:2], params[2:3]
        row, col = params[3:4] * (1.0 / GRID), params[4:5] * (1.0 / GRID)
        col_kernel = params[6:7].astype(jnp.int32)
        layer = params[7:8]
        fine_re[:, lanes], fine_im[:, lanes] = turn_cos_sin(row * fine_x)
        coarse_re[:, lanes], coarse_im[:, lanes] = turn_cos_sin(row * coarse_x)
        cf_re, cf_im = turn_cos_sin(col * fine_x)
        cc_re, cc_im = turn_cos_sin(col * pixel_y)
        cv_re = cc_re * vis_real - cc_im * vis_imag
        cv_im = cc_re * vis_imag + cc_im * vis_real
        masks = [
            jnp.broadcast_to(jnp.where(layer == float(item), 1.0, 0.0), (FINE, LANES))
            for item in range(layer_dev)
        ]
        index = jnp.broadcast_to(col_kernel, (FINE, LANES))
        for group in range(pixels // FINE):
            rows = slice(group * FINE, (group + 1) * FINE)
            k_re = jnp.take_along_axis(v_re[rows], index, axis=1, mode="promise_in_bounds")
            k_im = jnp.take_along_axis(v_im[rows], index, axis=1, mode="promise_in_bounds")
            e_re = cf_re * cv_re[group : group + 1] - cf_im * cv_im[group : group + 1]
            e_im = cf_re * cv_im[group : group + 1] + cf_im * cv_re[group : group + 1]
            real = e_re * k_re - e_im * k_im
            imag = e_re * k_im + e_im * k_re
            for item in range(layer_dev):
                for place, value in enumerate((real, imag)):
                    high, low = split(value * masks[item])
                    start = (item * 2 + place) * pixels + group * FINE
                    w_high[start : start + FINE, lanes] = high
                    w_low[start : start + FINE, lanes] = low
        return square + weight * weight

    squares = lax.fori_loop(0, tiles, prepare, jnp.zeros((1, LANES), jnp.float32))
    square_sum = jnp.sum(squares)

    y_pixel = first_pixel + lax.broadcasted_iota(jnp.int32, (1, pixels), 1)
    y_coord = (y_pixel - GRID // 2).astype(jnp.float32) * (field_of_view / GRID)
    top_depth = jnp.sqrt(1.0 - y_coord * y_coord) - 1.0
    for block in range(half // XBLOCK):

        def expand(tile, carry):
            lanes = pl.ds(pl.multiple_of(tile * LANES, LANES), LANES)
            params = slots_ref[tile]
            index = jnp.broadcast_to(params[5:6].astype(jnp.int32), (FINE, LANES))
            f_re, f_im = fine_re[:, lanes], fine_im[:, lanes]
            c_re, c_im = coarse_re[:, lanes], coarse_im[:, lanes]
            for group in range(XBLOCK // FINE):
                place = block * (XBLOCK // FINE) + group
                rows = slice(place * FINE, (place + 1) * FINE)
                k_re = jnp.take_along_axis(u_re[rows, :], index, axis=1, mode="promise_in_bounds")
                k_im = jnp.take_along_axis(u_im[rows, :], index, axis=1, mode="promise_in_bounds")
                g_re, g_im = c_re[place : place + 1], c_im[place : place + 1]
                e_re = f_re * g_re - f_im * g_im
                e_im = f_re * g_im + f_im * g_re
                real = e_re * k_re - e_im * k_im
                imag = e_re * k_im + e_im * k_re
                if place == 0:
                    odd = params[3:4].astype(jnp.int32) % 2
                    sign = (1 - 2 * odd).astype(jnp.float32)
                    first_row = lax.broadcasted_iota(jnp.int32, (FINE, LANES), 0) == 0
                    imag = imag * jnp.where(first_row, sign, 1.0)
                for part, value in enumerate((real, imag)):
                    high, low = split(value)
                    start = part * XBLOCK + group * FINE
                    lhs_high[start : start + FINE, lanes] = high
                    lhs_low[start : start + FINE, lanes] = low
            return carry

        lax.fori_loop(0, tiles, expand, 0)
        product = (
            dot_nt(lhs_high[...], w_high[...])
            + dot_nt(lhs_high[...], w_low[...])
            + dot_nt(lhs_low[...], w_high[...])
        )
        x_row = block * XBLOCK + lax.broadcasted_iota(jnp.int32, (XBLOCK, 1), 0)
        x_coord = (x_row - GRID // 2).astype(jnp.float32) * (field_of_view / GRID)
        depth = jnp.sqrt(1.0 - x_coord * x_coord - y_coord * y_coord) - 1.0
        above = jnp.zeros((XBLOCK, pixels), jnp.float32)
        below = jnp.zeros((XBLOCK, pixels), jnp.float32)
        for item in range(layer_dev):
            first = item * 2 * pixels
            p_ac = product[:XBLOCK, first : first + pixels]
            p_ad = product[:XBLOCK, first + pixels : first + 2 * pixels]
            p_bc = product[XBLOCK:, first : first + pixels]
            p_bd = product[XBLOCK:, first + pixels : first + 2 * pixels]
            cos_part, sin_part = turn_cos_sin(depth_ref[item] * depth)
            if block == 0:
                top = x_row == 0
                top_cos, top_sin = turn_cos_sin(depth_ref[item] * top_depth)
                top_value = p_bc * top_cos - p_bd * top_sin
                p_bc = jnp.where(top, 0.0, p_bc)
                p_bd = jnp.where(top, 0.0, p_bd)
            above += (p_ac - p_bd) * cos_part - (p_ad + p_bc) * sin_part
            lower = (p_ac + p_bd) * cos_part - (p_ad - p_bc) * sin_part
            if block == 0:
                lower = jnp.where(top, top_value, lower)
            below += lower
        neg[block * XBLOCK : (block + 1) * XBLOCK, :] = below
        position = block * XBLOCK
        owner, inside = position // chunk_rows, position % chunk_rows
        for part in range(max(1, XBLOCK // chunk_rows)):
            size = min(XBLOCK, chunk_rows)
            out_ref[owner + part, inside : inside + size, :] = above[part * size : (part + 1) * size]
    parts = blocks // 2
    for part in range(parts):
        target = blocks - 1 - part
        out_ref[target, 0:chunk_rows, :] = neg[part * chunk_rows : (part + 1) * chunk_rows, :]
        source = (part + 1) % parts * chunk_rows
        out_ref[target, 0:1, :] = neg[source : source + 1, :]
    for target in range(blocks):
        out_ref[target, chunk_rows:, :] = jnp.full((8, pixels), square_sum, jnp.float32)


def reduce_kernel(count, own_ref, out_ref, held, send_sem, recv_sem):
    me = lax.axis_index("wa")
    rows = out_ref.shape[0]
    greet("wa", me, count)
    copies = []
    for step in range(1, count):
        peer = lax.rem(me + step, count)
        copy = pltpu.make_async_remote_copy(
            src_ref=own_ref.at[peer],
            dst_ref=held.at[step - 1],
            send_sem=send_sem.at[step - 1],
            recv_sem=recv_sem.at[step - 1],
            device_id={"wa": peer},
            device_id_type=MESH,
        )
        copy.start()
        copies.append(copy)
    total = own_ref[me]
    for step, copy in enumerate(copies):
        copy.wait()
        total = total + held[step]
    value = total[:rows] / jnp.sqrt(total[rows : rows + 1])
    out_row = lax.broadcasted_iota(jnp.int32, (rows, rows), 0)
    in_row = lax.broadcasted_iota(jnp.int32, (rows, rows), 1)
    turned = jnp.where(me * 2 >= count, (rows - out_row) % rows, out_row)
    chosen = jnp.where(turned == in_row, 1.0, 0.0).astype(jnp.bfloat16)
    high, rest = split(value)
    low, last = split(value - high.astype(jnp.float32))
    out_ref[...] = sum(
        jnp.dot(chosen, piece, preferred_element_type=jnp.float32) for piece in (high, low, last)
    )


def body(
    visibilities,
    weights,
    cell_index,
    kernel_index,
    layer_index,
    tile_counts,
    kernel_table,
    layer_depth,
):
    layer_dev = layer_depth.shape[0]
    peers = lax.axis_size("bl")
    blocks = lax.axis_size("wa")
    pixels = GRID // peers
    chunk_rows = GRID // blocks
    tiles = cell_index.shape[1]
    position = lax.broadcasted_iota(jnp.int32, cell_index.shape, 2)
    used_weight = jnp.where(position < tile_counts[:, :, None], weights, 0.0)
    packed = jnp.stack(
        [
            visibilities[0, :, 0, :] * used_weight[0],
            visibilities[0, :, 1, :] * used_weight[0],
            used_weight[0],
            (cell_index[0] // GRID).astype(jnp.float32),
            (cell_index[0] % GRID).astype(jnp.float32),
            (kernel_index[0] // OVERSAMPLE).astype(jnp.float32),
            (kernel_index[0] % OVERSAMPLE).astype(jnp.float32),
            layer_index[0].astype(jnp.float32),
        ],
        axis=1,
    )
    vmem = pl.BlockSpec(memory_space=pltpu.VMEM)
    smem = pl.BlockSpec(memory_space=pltpu.SMEM)
    slots = pl.pallas_call(
        functools.partial(gather_kernel, peers),
        out_shape=jax.ShapeDtypeStruct((peers, tiles, 8, LANES), jnp.float32),
        in_specs=[vmem],
        out_specs=vmem,
        scratch_shapes=[
            pltpu.SemaphoreType.DMA((peers - 1,)),
            pltpu.SemaphoreType.DMA((peers - 1,)),
        ],
        compiler_params=pltpu.CompilerParams(collective_id=0, has_side_effects=True),
        name="gather_slots",
    )(packed)
    slots = slots.reshape(peers * tiles, 8, LANES)
    count = peers * tiles * LANES
    half = GRID // 2
    columns = 2 * layer_dev * pixels
    partial_image = pl.pallas_call(
        functools.partial(compute_kernel, layer_dev, pixels, blocks),
        out_shape=jax.ShapeDtypeStruct((blocks, chunk_rows + 8, pixels), jnp.float32),
        in_specs=[smem, vmem, vmem],
        out_specs=vmem,
        scratch_shapes=[
            pltpu.VMEM((LANES, LANES), jnp.float32),
            pltpu.VMEM((half, LANES), jnp.float32),
            pltpu.VMEM((half, LANES), jnp.float32),
            pltpu.VMEM((FINE, count), jnp.float32),
            pltpu.VMEM((FINE, count), jnp.float32),
            pltpu.VMEM((half // FINE, count), jnp.float32),
            pltpu.VMEM((half // FINE, count), jnp.float32),
            pltpu.VMEM((columns, count), jnp.bfloat16),
            pltpu.VMEM((columns, count), jnp.bfloat16),
            pltpu.VMEM((2 * XBLOCK, count), jnp.bfloat16),
            pltpu.VMEM((2 * XBLOCK, count), jnp.bfloat16),
            pltpu.VMEM((half, pixels), jnp.float32),
        ],
        compiler_params=pltpu.CompilerParams(vmem_limit_bytes=48 * 1024 * 1024),
        name="image_block",
    )(layer_depth, kernel_table, slots)
    return pl.pallas_call(
        functools.partial(reduce_kernel, blocks),
        out_shape=jax.ShapeDtypeStruct((chunk_rows, pixels), jnp.float32),
        in_specs=[vmem],
        out_specs=vmem,
        scratch_shapes=[
            pltpu.VMEM((blocks - 1, chunk_rows + 8, pixels), jnp.float32),
            pltpu.SemaphoreType.DMA((blocks - 1,)),
            pltpu.SemaphoreType.DMA((blocks - 1,)),
        ],
        compiler_params=pltpu.CompilerParams(collective_id=1, has_side_effects=True),
        name="sum_layers",
    )(partial_image)


def solution(mesh):
    in_specs = (
        P("wa", "bl", None, None),
        P("wa", "bl", None),
        P("wa", "bl", None),
        P("wa", "bl", None),
        P("wa", "bl", None),
        P("wa", "bl"),
        P(),
        P("wa"),
    )
    out_specs = P("wa", "bl")
    return jax.shard_map(body, mesh=mesh, in_specs=in_specs, out_specs=out_specs, check_vma=False)
```

profile of v0, /device:TPU:0, one launch (start us, length us, event | category | flops | bytes accessed | tf_op | source)
XLA Modules:
  0.0 50.7 jit_solution(8805735416579341816)
XLA Ops:
  0.0 0.0 copy-start.7
  0.0 0.0 copy-start.9
  0.0 0.7 %copy-done.7 = f32[1,2,128]{2,1,0:T(2,128)S(1)} copy-done((f32[1,2,128]{2,1,0:T(2,128)S(1)}, f32[1,2,128]{2,1,0:T(2,128)}, u32[]{:S(2)}) %copy-start.7) | copy-done | bytes 1048
  0.7 0.0 copy-done.9
  0.7 0.1 compare_select_fusion.6
  0.8 0.0 copy-start.8
  0.8 0.7 %copy-done.8 = s32[1,2,128]{2,1,0:T(2,128)S(1)} copy-done((s32[1,2,128]{2,1,0:T(2,128)S(1)}, s32[1,2,128]{2,1,0:T(2,128)}, u32[]{:S(2)}) %copy-start.8) | copy-done | bytes 1048
  1.4 0.0 copy-start.6
  1.4 0.7 %copy-done.6 = f32[1,2,2,128]{3,2,1,0:T(2,128)S(1)} copy-done((f32[1,2,2,128]{3,2,1,0:T(2,128)S(1)}, f32[1,2,2,128]{3,2,1,0:T(2,128)}, u32[]{:S(2)}) %copy-start.6) | copy-done | bytes 2072
  2.1 0.7 %copy-done.5 = s32[1,2,128]{2,1,0:T(2,128)S(1)} copy-done((s32[1,2,128]{2,1,0:T(2,128)S(1)}, s32[1,2,128]{2,1,0:T(2,128)}, u32[]{:S(2)}) %copy-start.5) | copy-done | bytes 1048
  2.8 0.0 copy-done.4
  2.9 0.0 copy-start.3
  2.9 0.6 %stack.2.own_ref = f32[2,8,128]{2,1,0:T(8,128)} concatenate(f32[2,1,128]{2,1,0:T(1,128)S(1)} %get-tuple-element.10, f32[2,1,128]{2,1,0:T(1,128)S(1)} %get-tuple-element.9, f32[2,1,128]{2,1,0:T(1,128)S(1)} %bitcast.16, f32[2,1,128]{2,1,0:T(1,128)S(1)} %fusion.2, f32[2,1,128]{2,1,0:T(1,128)S(1)} %get-tuple-element.7, f32[2,1,128]{2,1,0:T(1,128)S(1)} %fusion.3, ...), dimensions={1} | concatenate | bytes 16384 | tf_op jit(solution)/shard_map/stack | solution.py:301
  3.5 0.1 copy-done.3
  3.6 0.1 copy.11.table_ref
  3.6 7.7 %gather_slots.1 = f32[8,2,8,128]{3,2,1,0:T(8,128)} custom-call(f32[2,8,128]{2,1,0:T(8,128)} %stack.2.own_ref), custom_call_target="tpu_custom_call" | custom-call | tf_op jit(solution)/shard_map/gather_slots/pallas_call | solution.py:316
  11.4 0.0 copy-start.2
  11.4 0.6 %copy-done.2 = f32[2]{0:T(128)S(1)} copy-done((f32[2]{0:T(128)S(1)}, f32[2]{0:T(128)}, u32[]{:S(2)}) %copy-start.2) | copy-done | bytes 32
  12.0 0.8 %copy-done.1 = f32[8,2,8,128]{3,2,1,0:T(8,128)S(1)} copy-done((f32[8,2,8,128]{3,2,1,0:T(8,128)S(1)}, f32[8,2,8,128]{3,2,1,0:T(8,128)}, u32[]{:S(2)}) %copy-start.1) | copy-done | bytes 65560
  12.9 19.8 %image_block.1.own_ref = f32[4,264,128]{2,1,0:T(8,128)S(1)} custom-call(f32[2]{0:T(128)S(1)} %copy-done.2, f32[16,8]{1,0:T(8,128)S(1)} %copy.11.table_ref, f32[16,8,128]{2,1,0:T(8,128)S(1)} %bitcast.14), custom_call_target="tpu_custom_call" | custom-call | tf_op jit(solution)/shard_map/image_block/pallas_call | solution.py:332
  32.7 0.0 copy-start
  32.7 0.8 %copy-done = f32[4,264,128]{2,1,0:T(8,128)} copy-done((f32[4,264,128]{2,1,0:T(8,128)}, f32[4,264,128]{2,1,0:T(8,128)S(1)}, u32[]{:S(2)}) %copy-start) | copy-done | bytes 540696
  33.5 15.6 %sum_layers.1 = f32[256,128]{1,0:T(8,128)} custom-call(f32[4,264,128]{2,1,0:T(8,128)} %copy-done), custom_call_target="tpu_custom_call" | custom-call | tf_op jit(solution)/shard_map/sum_layers/pallas_call | solution.py:354
  49.1 1.6 %copy.15 = f32[256,128]{1,0:T(8,128)} copy(f32[256,128]{1,0:T(8,128)} %sum_layers.1) | data formatting | bytes 262144
  (8 shorter events, 0.0 us)
Async XLA Ops:
  0.0 0.7 %copy-start.7 = (f32[1,2,128]{2,1,0:T(2,128)S(1)}, f32[1,2,128]{2,1,0:T(2,128)}, u32[]{:S(2)}) copy-start(f32[1,2,128]{2,1,0:T(2,128)} %param.9) | copy-start | bytes 3076
  0.0 0.7 %copy-start.9 = (s32[1,2]{1,0:T(1,128)S(1)}, s32[1,2]{1,0:T(1,128)}, u32[]{:S(2)}) copy-start(s32[1,2]{1,0:T(1,128)} %param.13) | copy-start | bytes 28
  0.8 0.7 %copy-start.8 = (s32[1,2,128]{2,1,0:T(2,128)S(1)}, s32[1,2,128]{2,1,0:T(2,128)}, u32[]{:S(2)}) copy-start(s32[1,2,128]{2,1,0:T(2,128)} %param.12) | copy-start | bytes 3076
  1.4 0.7 %copy-start.6 = (f32[1,2,2,128]{3,2,1,0:T(2,128)S(1)}, f32[1,2,2,128]{3,2,1,0:T(2,128)}, u32[]{:S(2)}) copy-start(f32[1,2,2,128]{3,2,1,0:T(2,128)} %param.8) | copy-start | bytes 6148
  2.1 0.7 %copy-start.5 = (s32[1,2,128]{2,1,0:T(2,128)S(1)}, s32[1,2,128]{2,1,0:T(2,128)}, u32[]{:S(2)}) copy-start(s32[1,2,128]{2,1,0:T(2,128)} %param.11) | copy-start | bytes 3076
  2.1 0.7 %copy-start.4 = (s32[1,2,128]{2,1,0:T(2,128)S(1)}, s32[1,2,128]{2,1,0:T(2,128)}, u32[]{:S(2)}) copy-start(s32[1,2,128]{2,1,0:T(2,128)} %param.10) | copy-start | bytes 3076
  2.9 0.7 %copy-start.3 = (f32[16,8]{0,1:T(8,128)S(1)}, f32[16,8]{0,1:T(8,128)}, u32[]{:S(2)}) copy-start(f32[16,8]{0,1:T(8,128)} %param.14) | copy-start | bytes 1540
  11.4 0.7 %copy-start.2 = (f32[2]{0:T(128)S(1)}, f32[2]{0:T(128)}, u32[]{:S(2)}) copy-start(f32[2]{0:T(128)} %depth_ref.1) | copy-start | bytes 28
  12.0 0.8 %copy-start.1 = (f32[8,2,8,128]{3,2,1,0:T(8,128)S(1)}, f32[8,2,8,128]{3,2,1,0:T(8,128)}, u32[]{:S(2)}) copy-start(f32[8,2,8,128]{3,2,1,0:T(8,128)} %gather_slots.1) | copy-start | bytes 196612
  32.7 0.8 %copy-start = (f32[4,264,128]{2,1,0:T(8,128)}, f32[4,264,128]{2,1,0:T(8,128)S(1)}, u32[]{:S(2)}) copy-start(f32[4,264,128]{2,1,0:T(8,128)S(1)} %image_block.1.own_ref) | copy-start | bytes 1622020
where the time goes:
time: 51.6 us; the launch traced here: 50.7 us
  Pallas kernels  43.1 us (84%)
  local copies, waits for them, and re-layouts  7.34 us (14%)
    pallas_call x1, Pallas kernels, body(): pl.pallas_call(functools.partial(compute_kernel, layer_dev, pixels, block...  19.8 us
    pallas_call x1, Pallas kernels, body(): pl.pallas_call(functools.partial(reduce_kernel, blocks), out_shape=jax.Sh...  15.6 us
    pallas_call x1, Pallas kernels, body(): pl.pallas_call(functools.partial(gather_kernel, peers), out_shape=jax.Sha...  7.73 us
    unnamed x22, local copies, waits for them, and re-layouts  6.72 us

commit v1 on v0

v1 whole, which is shorter than its diff:
```python
import functools
import math

import jax
import jax.numpy as jnp
from jax import lax
from jax.experimental import pallas as pl
from jax.experimental.pallas import tpu as pltpu
from jax.sharding import PartitionSpec as P

GRID = 1024
SUPPORT = 8
OVERSAMPLE = 16
LANES = 128
FINE = 32
XBLOCK = 128
CHUNK = 2 * LANES
PIECES = 3

field_of_view = 0.6
MESH = pl.DeviceIdType.MESH

TWO_PI = 2.0 * math.pi
SIN_TERMS = [(-1) ** k * TWO_PI ** (2 * k + 1) / math.factorial(2 * k + 1) for k in range(9)]
COS_TERMS = [(-1) ** k * TWO_PI ** (2 * k) / math.factorial(2 * k) for k in range(10)]


def horner(square, terms):
    value = jnp.full_like(square, terms[-1])
    for term in terms[-2::-1]:
        value = value * square + term
    return value


def turn_cos_sin(turns):
    part = turns - jnp.round(turns)
    square = part * part
    return horner(square, COS_TERMS), part * horner(square, SIN_TERMS)


def split(value):
    high = value.astype(jnp.bfloat16)
    return high, (value - high.astype(jnp.float32)).astype(jnp.bfloat16)


def dot_nt(a, b):
    return lax.dot_general(
        a, b, (((1,), (1,)), ((), ())), preferred_element_type=jnp.float32
    )


def factor_table(first, rows, table, special):
    pixel = (first + lax.broadcasted_iota(jnp.int32, (rows, LANES), 0)).astype(jnp.float32)
    offset_lane = lax.broadcasted_iota(jnp.int32, (rows, LANES), 1)
    offset = (offset_lane % SUPPORT - SUPPORT // 2).astype(jnp.float32)
    cos_part, sin_part = turn_cos_sin(pixel * offset * (1.0 / GRID))
    if special:
        row = lax.broadcasted_iota(jnp.int32, (rows, LANES), 0)
        parity = 1.0 - 2.0 * (offset_lane % 2).astype(jnp.float32)
        sin_part = jnp.where(row == 0, parity, sin_part)
    table_high, table_low = split(table)

    def product(part):
        high, low = split(part)
        return dot_nt(high, table_high) + dot_nt(high, table_low) + dot_nt(low, table_high)

    return product(cos_part), product(sin_part)


def start_all(copies):
    for copy in copies:
        copy.start()


def kernel(
    layer_dev,
    pixels,
    blocks,
    peers,
    depth_ref,
    counts_ref,
    table_ref,
    vis_ref,
    weight_ref,
    cell_ref,
    index_ref,
    layer_ref,
    out_ref,
    own,
    slots_ref,
    table_pad,
    u_re,
    u_im,
    v_re,
    v_im,
    fine_re,
    fine_im,
    coarse_re,
    coarse_im,
    rhs,
    lhs,
    acc,
    image,
    tail,
    held,
    held_tail,
    slot_send,
    slot_recv,
    image_send,
    image_recv,
    tail_send,
    tail_recv,
):
    half = GRID // 2
    chunk_rows = GRID // blocks
    own_tiles = own.shape[0]
    tiles = peers * own_tiles
    block_total = half // XBLOCK
    subs = chunk_rows // XBLOCK
    me_bl, me_wa = lax.axis_index("bl"), lax.axis_index("wa")
    barrier = pltpu.get_barrier_semaphore()
    for axis, me, count in (("bl", me_bl, peers), ("wa", me_wa, blocks)):
        for step in range(1, count):
            pl.semaphore_signal(
                barrier, inc=1, device_id={axis: lax.rem(me + step, count)}, device_id_type=MESH
            )
    position = lax.broadcasted_iota(jnp.int32, (1, LANES), 1)
    for tile in range(own_tiles):
        line = slice(tile, tile + 1)
        weight = jnp.where(position < counts_ref[0, tile], weight_ref[0, line], 0.0)
        cell, index = cell_ref[0, line], index_ref[0, line]
        values = [
            vis_ref[0, tile, 0:1] * weight,
            vis_ref[0, tile, 1:2] * weight,
            weight,
            (cell // GRID).astype(jnp.float32),
            (cell % GRID).astype(jnp.float32),
            (index // OVERSAMPLE).astype(jnp.float32),
            (index % OVERSAMPLE).astype(jnp.float32),
            layer_ref[0, line].astype(jnp.float32),
        ]
        for place, value in enumerate(values):
            own[tile, place : place + 1] = value
    pl.semaphore_wait(barrier, peers + blocks - 2)
    slot_copies = [
        pltpu.make_async_remote_copy(
            src_ref=own,
            dst_ref=slots_ref.at[pl.ds(me_bl * own_tiles, own_tiles)],
            send_sem=slot_send.at[step - 1],
            recv_sem=slot_recv.at[step - 1],
            device_id={"bl": lax.rem(me_bl + step, peers)},
            device_id_type=MESH,
        )
        for step in range(1, peers)
    ]
    start_all(slot_copies)
    slots_ref[pl.ds(me_bl * own_tiles, own_tiles)] = own[...]

    first_pixel = me_bl * pixels
    table_pad[...] = jnp.zeros_like(table_pad)
    table_pad[0:OVERSAMPLE, 0:SUPPORT] = table_ref[...]
    table = table_pad[...]
    u_re[...], u_im[...] = factor_table(0, half, table, True)
    v_re[...], v_im[...] = factor_table(first_pixel, pixels, table, False)
    fine_x = lax.broadcasted_iota(jnp.int32, (FINE, LANES), 0).astype(jnp.float32)
    coarse_x = (lax.broadcasted_iota(jnp.int32, (half // FINE, LANES), 0) * FINE).astype(
        jnp.float32
    )
    pixel_y = (
        first_pixel + lax.broadcasted_iota(jnp.int32, (pixels // FINE, LANES), 0) * FINE
    ).astype(jnp.float32)
    for copy in slot_copies:
        copy.wait()

    def lanes_of(tile):
        return pl.ds(pl.multiple_of(tile * LANES, LANES), LANES)

    def piece_lanes(tile):
        base = tile // 2 * (PIECES * CHUNK) + tile % 2 * LANES
        return [
            pl.ds(pl.multiple_of(base + piece * CHUNK, LANES), LANES) for piece in range(PIECES)
        ]

    def prepare(tile, square):
        lanes = lanes_of(tile)
        places = piece_lanes(tile)
        params = slots_ref[tile]
        vis_real, vis_imag, weight = params[0:1], params[1:2], params[2:3]
        row, col = params[3:4] * (1.0 / GRID), params[4:5] * (1.0 / GRID)
        col_kernel = params[6:7].astype(jnp.int32)
        layer = params[7:8]
        fine_re[:, lanes], fine_im[:, lanes] = turn_cos_sin(row * fine_x)
        coarse_re[:, lanes], coarse_im[:, lanes] = turn_cos_sin(row * coarse_x)
        cf_re, cf_im = turn_cos_sin(col * fine_x)
        cc_re, cc_im = turn_cos_sin(col * pixel_y)
        cv_re = cc_re * vis_real - cc_im * vis_imag
        cv_im = cc_re * vis_imag + cc_im * vis_real
        masks = [
            jnp.broadcast_to(jnp.where(layer == float(item), 1.0, 0.0), (FINE, LANES))
            for item in range(layer_dev)
        ]
        index = jnp.broadcast_to(col_kernel, (FINE, LANES))
        for group in range(pixels // FINE):
            rows = slice(group * FINE, (group + 1) * FINE)
            k_re = jnp.take_along_axis(v_re[rows, :], index, axis=1, mode="promise_in_bounds")
            k_im = jnp.take_along_axis(v_im[rows, :], index, axis=1, mode="promise_in_bounds")
            e_re = cf_re * cv_re[group : group + 1] - cf_im * cv_im[group : group + 1]
            e_im = cf_re * cv_im[group : group + 1] + cf_im * cv_re[group : group + 1]
            real = e_re * k_re - e_im * k_im
            imag = e_re * k_im + e_im * k_re
            for item in range(layer_dev):
                for place, value in enumerate((real, imag)):
                    high, low = split(value * masks[item])
                    start = (item * 2 + place) * pixels + group * FINE
                    for where, piece in zip(places, (high, low, high)):
                        rhs[start : start + FINE, where] = piece
        return square + weight * weight

    squares = lax.fori_loop(0, tiles, prepare, jnp.zeros((1, LANES), jnp.float32))
    square_sum = jnp.sum(squares)

    def expand(block, tile):
        lanes = lanes_of(tile)
        places = piece_lanes(tile)
        params = slots_ref[tile]
        index = jnp.broadcast_to(params[5:6].astype(jnp.int32), (FINE, LANES))
        f_re, f_im = fine_re[:, lanes], fine_im[:, lanes]
        for group in range(XBLOCK // FINE):
            place = block * (XBLOCK // FINE) + group
            rows = slice(place * FINE, (place + 1) * FINE)
            k_re = jnp.take_along_axis(u_re[rows, :], index, axis=1, mode="promise_in_bounds")
            k_im = jnp.take_along_axis(u_im[rows, :], index, axis=1, mode="promise_in_bounds")
            g_re = coarse_re[place : place + 1, lanes]
            g_im = coarse_im[place : place + 1, lanes]
            e_re = f_re * g_re - f_im * g_im
            e_im = f_re * g_im + f_im * g_re
            real = e_re * k_re - e_im * k_im
            imag = e_re * k_im + e_im * k_re
            if place == 0:
                odd = params[3:4].astype(jnp.int32) % 2
                sign = (1 - 2 * odd).astype(jnp.float32)
                first_row = lax.broadcasted_iota(jnp.int32, (FINE, LANES), 0) == 0
                imag = imag * jnp.where(first_row, sign, 1.0)
            for part, value in enumerate((real, imag)):
                high, low = split(value)
                start = part * XBLOCK + group * FINE
                for where, piece in zip(places, (high, high, low)):
                    lhs[block % 2, start : start + FINE, where] = piece

    def image_copy(owner, sub):
        slot = lax.rem(owner - me_wa + blocks, blocks) - 1
        rows = pl.ds(sub * XBLOCK, XBLOCK)
        return pltpu.make_async_remote_copy(
            src_ref=image.at[owner, rows],
            dst_ref=held.at[slot, rows],
            send_sem=image_send.at[owner, sub],
            recv_sem=image_recv.at[slot, sub],
            device_id={"wa": owner},
            device_id_type=MESH,
        )

    def tail_copy(step):
        peer = lax.rem(me_wa + step, blocks)
        return pltpu.make_async_remote_copy(
            src_ref=tail.at[peer],
            dst_ref=held_tail.at[step - 1],
            send_sem=tail_send.at[step - 1],
            recv_sem=tail_recv.at[step - 1],
            device_id={"wa": peer},
            device_id_type=MESH,
        )

    y_pixel = first_pixel + lax.broadcasted_iota(jnp.int32, (1, pixels), 1)
    y_coord = (y_pixel - GRID // 2).astype(jnp.float32) * (field_of_view / GRID)
    top_depth = jnp.sqrt(1.0 - y_coord * y_coord) - 1.0
    tail[...] = jnp.full_like(tail, square_sum)

    @pl.loop(0, tiles)
    def _(tile):
        expand(0, tile)

    parts = blocks // 2
    for block in range(block_total):

        @pl.loop(0, tiles // 2)
        def _(chunk):
            wide = pl.ds(pl.multiple_of(chunk * (PIECES * CHUNK), LANES), PIECES * CHUNK)
            product = dot_nt(lhs[block % 2, :, wide], rhs[:, wide])
            if block + 1 < block_total:
                expand(block + 1, chunk * 2)
                expand(block + 1, chunk * 2 + 1)
            acc[...] = jnp.where(chunk == 0, 0.0, acc[...]) + product

        x_row = block * XBLOCK + lax.broadcasted_iota(jnp.int32, (XBLOCK, 1), 0)
        x_coord = (x_row - GRID // 2).astype(jnp.float32) * (field_of_view / GRID)
        depth = jnp.sqrt(1.0 - x_coord * x_coord - y_coord * y_coord) - 1.0
        above = jnp.zeros((XBLOCK, pixels), jnp.float32)
        below = jnp.zeros((XBLOCK, pixels), jnp.float32)
        for item in range(layer_dev):
            first = item * 2 * pixels
            p_ac = acc[:XBLOCK, first : first + pixels]
            p_ad = acc[:XBLOCK, first + pixels : first + 2 * pixels]
            p_bc = acc[XBLOCK:, first : first + pixels]
            p_bd = acc[XBLOCK:, first + pixels : first + 2 * pixels]
            cos_part, sin_part = turn_cos_sin(depth_ref[item] * depth)
            if block == 0:
                top = x_row == 0
                top_cos, top_sin = turn_cos_sin(depth_ref[item] * top_depth)
                top_value = p_bc * top_cos - p_bd * top_sin
                p_bc = jnp.where(top, 0.0, p_bc)
                p_bd = jnp.where(top, 0.0, p_bd)
            above += (p_ac - p_bd) * cos_part - (p_ad + p_bc) * sin_part
            lower = (p_ac + p_bd) * cos_part - (p_ad - p_bc) * sin_part
            if block == 0:
                lower = jnp.where(top, top_value, lower)
            below += lower
        part, sub = block // subs, block % subs
        rows = slice(sub * XBLOCK, (sub + 1) * XBLOCK)
        for owner, value in ((part, above), (blocks - 1 - part, below)):
            image[owner, rows, :] = value

            @pl.when(me_wa != owner)
            def _():
                image_copy(owner, sub).start()

        if sub == 0:
            target = blocks - 1 - (part - 1) % parts
            tail[target, 1:2, :] = below[0:1]

    tail_copies = [tail_copy(step) for step in range(1, blocks)]
    start_all(tail_copies)
    total = image[me_wa]
    total_tail = tail[me_wa]
    for step in range(1, blocks):
        for sub in range(subs):
            rows = pl.ds(sub * XBLOCK, XBLOCK)
            pltpu.make_async_remote_copy(
                src_ref=image.at[me_wa, rows],
                dst_ref=held.at[step - 1, rows],
                send_sem=image_send.at[me_wa, sub],
                recv_sem=image_recv.at[step - 1, sub],
                device_id={"wa": lax.rem(me_wa + step, blocks)},
                device_id_type=MESH,
            ).wait_recv()
        total = total + held[step - 1]
    for step, copy in enumerate(tail_copies):
        copy.wait()
        total_tail = total_tail + held_tail[step]
    scale = 1.0 / jnp.sqrt(total_tail[0:1])
    out_row = lax.broadcasted_iota(jnp.int32, (chunk_rows, chunk_rows), 0)
    in_row = lax.broadcasted_iota(jnp.int32, (chunk_rows, chunk_rows), 1)
    mirrored = me_wa * 2 >= blocks
    turned = jnp.where(mirrored, (chunk_rows - out_row) % chunk_rows, out_row)
    chosen = jnp.where(turned == in_row, 1.0, 0.0).astype(jnp.bfloat16)
    high, rest = split(total)
    low, last = split(total - high.astype(jnp.float32))
    ordered = sum(
        jnp.dot(chosen, piece, preferred_element_type=jnp.float32) for piece in (high, low, last)
    )
    out_line = lax.broadcasted_iota(jnp.int32, (chunk_rows, 1), 0)
    swap = jnp.where(mirrored, out_line, 1) == 0
    out_ref[...] = jnp.where(swap, total_tail[1:2], ordered) * scale
    for owner in range(blocks):

        @pl.when(me_wa != owner)
        def _():
            for sub in range(subs):
                image_copy(owner, sub).wait_send()


def body(
    visibilities,
    weights,
    cell_index,
    kernel_index,
    layer_index,
    tile_counts,
    kernel_table,
    layer_depth,
):
    layer_dev = layer_depth.shape[0]
    peers = lax.axis_size("bl")
    blocks = lax.axis_size("wa")
    pixels = GRID // peers
    chunk_rows = GRID // blocks
    own_tiles = cell_index.shape[1]
    tiles = peers * own_tiles
    count = tiles * LANES
    half = GRID // 2
    columns = 2 * layer_dev * pixels
    vmem = pl.BlockSpec(memory_space=pltpu.VMEM)
    smem = pl.BlockSpec(memory_space=pltpu.SMEM)
    f32, bf16 = jnp.float32, jnp.bfloat16
    shapes = [
        ((own_tiles, 8, LANES), f32),
        ((tiles, 8, LANES), f32),
        ((LANES, LANES), f32),
        ((half, LANES), f32),
        ((half, LANES), f32),
        ((pixels, LANES), f32),
        ((pixels, LANES), f32),
        ((FINE, count), f32),
        ((FINE, count), f32),
        ((half // FINE, count), f32),
        ((half // FINE, count), f32),
        ((columns, PIECES * count), bf16),
        ((2, 2 * XBLOCK, PIECES * count), bf16),
        ((2 * XBLOCK, columns), f32),
        ((blocks, chunk_rows, pixels), f32),
        ((blocks, 8, pixels), f32),
        ((blocks - 1, chunk_rows, pixels), f32),
        ((blocks - 1, 8, pixels), f32),
    ]
    subs = chunk_rows // XBLOCK
    semaphores = [
        (peers - 1,),
        (peers - 1,),
        (blocks, subs),
        (blocks - 1, subs),
        (blocks - 1,),
        (blocks - 1,),
    ]
    return pl.pallas_call(
        functools.partial(kernel, layer_dev, pixels, blocks, peers),
        out_shape=jax.ShapeDtypeStruct((chunk_rows, pixels), f32),
        in_specs=[smem, smem] + [vmem] * 6,
        out_specs=vmem,
        scratch_shapes=[pltpu.VMEM(shape, kind) for shape, kind in shapes]
        + [pltpu.SemaphoreType.DMA(shape) for shape in semaphores],
        compiler_params=pltpu.CompilerParams(
            collective_id=0, has_side_effects=True, vmem_limit_bytes=48 * 1024 * 1024
        ),
        name="dirty_image",
    )(
        layer_depth,
        tile_counts,
        kernel_table,
        visibilities,
        weights,
        cell_index,
        kernel_index,
        layer_index,
    )


def solution(mesh):
    in_specs = (
        P("wa", "bl", None, None),
        P("wa", "bl", None),
        P("wa", "bl", None),
        P("wa", "bl", None),
        P("wa", "bl", None),
        P("wa", "bl"),
        P(),
        P("wa"),
    )
    out_specs = P("wa", "bl")
    return jax.shard_map(body, mesh=mesh, in_specs=in_specs, out_specs=out_specs, check_vma=False)
```

time: 51.6 us -> 35.3 us (0.68); the launches traced: 50.7 us -> 35.2 us
  Pallas kernels: 43.1 us -> 33.6 us
  local copies, waits for them, and re-layouts: 7.34 us -> 1.52 us
    pallas_call x3 -> x1, Pallas kernels: 43.1 us -> 33.6 us  [body(): pl.pallas_call(functools.partial(kernel, layer_dev, pixels, blocks, peers...]
    unnamed x22 -> x16, local copies, waits for them, and re-layouts: 6.72 us -> 1.52 us
    another operation x1 -> x0, local copies, waits for them, and re-layouts: 0.62 us -> none  [body(): jnp.stack([visibilities[0, :, 0, :] * used_weight[0], visibilities[0, :,...]
where the time goes in v1:
time: 35.3 us; the launch traced here: 35.2 us
  Pallas kernels  33.6 us (95%)
  local copies, waits for them, and re-layouts  1.52 us (4%)
    pallas_call x1, Pallas kernels, body(): pl.pallas_call(functools.partial(kernel, layer_dev, pixels, blocks, peers...  33.6 us
    unnamed x16, local copies, waits for them, and re-layouts  1.52 us

profile of v1, /device:TPU:0, one launch (start us, length us, event | category | flops | bytes accessed | tf_op | source)
XLA Modules:
  0.0 35.2 jit_solution(3266229563956218332)
XLA Ops:
  0.0 0.0 copy-start.5
  0.0 0.0 copy-start.6
  0.0 0.0 copy-start.4
  0.0 0.0 copy-start.3
  0.0 0.0 copy-start.2
  0.0 0.0 copy-start.1
  0.0 0.0 copy-start
  0.0 0.8 %copy.9.table_ref = f32[16,8]{1,0:T(8,128)S(1)} copy(f32[16,8]{0,1:T(8,128)} %param.14) | data formatting | bytes 1024 | tf_op args[6]
  0.9 0.0 copy-done.5
  0.9 0.0 copy-done.6
  0.9 0.0 copy-done.4
  0.9 0.0 copy-done.3
  0.9 0.0 copy-done.2
  0.9 0.0 copy-done.1
  0.9 0.0 copy-done
  0.9 33.6 %dirty_image.1 = f32[256,128]{1,0:T(8,128)S(1)} custom-call(f32[2]{0:T(128)S(1)} %copy-done.5, s32[1,2]{1,0:T(1,128)S(1)} %copy-done.6, f32[16,8]{1,0:T(8,128)S(1)} %copy.9.table_ref, f32[1,2,2,128]{3,2,1,0:T(2,128)S(1)} %copy-done, f32[1,2,128]{2,1,0:T(2,128)S(1)} %copy-done.1, s32[1,2,128]{2,1,0:T(2,128)S(1)} %copy-done.2, s32[1,2,128]{2,1,0:T(2,128)S(1)} %copy-done.3, ...), custom_call_target="tpu_custom_call" | custom-call | tf_op jit(solution)/shard_map/dirty_image/pallas_call | solution.py:423
  34.5 0.7 %copy.11 = f32[256,128]{1,0:T(8,128)} copy(f32[256,128]{1,0:T(8,128)S(1)} %dirty_image.1) | data formatting | bytes 262144
Async XLA Ops:
  0.0 0.9 %copy-start.5 = (f32[2]{0:T(128)S(1)}, f32[2]{0:T(128)}, u32[]{:S(2)}) copy-start(f32[2]{0:T(128)} %depth_ref.1) | copy-start | bytes 28
  0.0 0.9 %copy-start.6 = (s32[1,2]{1,0:T(1,128)S(1)}, s32[1,2]{1,0:T(1,128)}, u32[]{:S(2)}) copy-start(s32[1,2]{1,0:T(1,128)} %counts_ref.1) | copy-start | bytes 28
  0.0 0.9 %copy-start.4 = (s32[1,2,128]{2,1,0:T(2,128)S(1)}, s32[1,2,128]{2,1,0:T(2,128)}, u32[]{:S(2)}) copy-start(s32[1,2,128]{2,1,0:T(2,128)} %layer_ref.1) | copy-start | bytes 3076
  0.0 0.9 %copy-start.3 = (s32[1,2,128]{2,1,0:T(2,128)S(1)}, s32[1,2,128]{2,1,0:T(2,128)}, u32[]{:S(2)}) copy-start(s32[1,2,128]{2,1,0:T(2,128)} %index_ref.1) | copy-start | bytes 3076
  0.0 0.9 %copy-start.2 = (s32[1,2,128]{2,1,0:T(2,128)S(1)}, s32[1,2,128]{2,1,0:T(2,128)}, u32[]{:S(2)}) copy-start(s32[1,2,128]{2,1,0:T(2,128)} %cell_ref.1) | copy-start | bytes 3076
  0.0 0.9 %copy-start.1 = (f32[1,2,128]{2,1,0:T(2,128)S(1)}, f32[1,2,128]{2,1,0:T(2,128)}, u32[]{:S(2)}) copy-start(f32[1,2,128]{2,1,0:T(2,128)} %weight_ref.1) | copy-start | bytes 3076
  0.0 0.9 %copy-start = (f32[1,2,2,128]{3,2,1,0:T(2,128)S(1)}, f32[1,2,2,128]{3,2,1,0:T(2,128)}, u32[]{:S(2)}) copy-start(f32[1,2,2,128]{3,2,1,0:T(2,128)} %vis_ref.1) | copy-start | bytes 6148

commit v2 on v1

--- a/solution.py
+++ b/solution.py
@@ -62,9 +62,13 @@
 
     def product(part):
         high, low = split(part)
-        return dot_nt(high, table_high) + dot_nt(high, table_low) + dot_nt(low, table_high)
+        return dot_nn(high, table_high) + dot_nn(high, table_low) + dot_nn(low, table_high)
 
     return product(cos_part), product(sin_part)
+
+
+def dot_nn(a, b):
+    return jnp.dot(a, b, preferred_element_type=jnp.float32)
 
 
 def start_all(copies):
@@ -77,6 +81,15 @@
     pixels,
     blocks,
     peers,
+    depth_hbm,
+    counts_hbm,
+    table_hbm,
+    vis_hbm,
+    weight_hbm,
+    cell_hbm,
+    index_hbm,
+    layer_hbm,
+    out_ref,
     depth_ref,
     counts_ref,
     table_ref,
@@ -85,7 +98,7 @@
     cell_ref,
     index_ref,
     layer_ref,
-    out_ref,
+    load_sem,
     own,
     slots_ref,
     table_pad,
@@ -118,16 +131,34 @@
     block_total = half // XBLOCK
     subs = chunk_rows // XBLOCK
     me_bl, me_wa = lax.axis_index("bl"), lax.axis_index("wa")
+    loads = [
+        pltpu.make_async_copy(source, target, load_sem.at[place])
+        for place, (source, target) in enumerate(
+            (
+                (counts_hbm, counts_ref),
+                (vis_hbm, vis_ref),
+                (weight_hbm, weight_ref),
+                (cell_hbm, cell_ref),
+                (index_hbm, index_ref),
+                (layer_hbm, layer_ref),
+                (table_hbm, table_ref),
+                (depth_hbm, depth_ref),
+            )
+        )
+    ]
+    start_all(loads)
     barrier = pltpu.get_barrier_semaphore()
     for axis, me, count in (("bl", me_bl, peers), ("wa", me_wa, blocks)):
         for step in range(1, count):
             pl.semaphore_signal(
                 barrier, inc=1, device_id={axis: lax.rem(me + step, count)}, device_id_type=MESH
             )
+    for load in loads:
+        load.wait()
     position = lax.broadcasted_iota(jnp.int32, (1, LANES), 1)
     for tile in range(own_tiles):
         line = slice(tile, tile + 1)
-        weight = jnp.where(position < counts_ref[0, tile], weight_ref[0, line], 0.0)
+        weight = jnp.where(position < counts_ref[0:1, tile : tile + 1], weight_ref[0, line], 0.0)
         cell, index = cell_ref[0, line], index_ref[0, line]
         values = [
             vis_ref[0, tile, 0:1] * weight,
@@ -158,7 +189,7 @@
 
     first_pixel = me_bl * pixels
     table_pad[...] = jnp.zeros_like(table_pad)
-    table_pad[0:OVERSAMPLE, 0:SUPPORT] = table_ref[...]
+    table_pad[0:SUPPORT, 0:OVERSAMPLE] = table_ref[...]
     table = table_pad[...]
     u_re[...], u_im[...] = factor_table(0, half, table, True)
     v_re[...], v_im[...] = factor_table(first_pixel, pixels, table, False)
@@ -219,7 +250,7 @@
     squares = lax.fori_loop(0, tiles, prepare, jnp.zeros((1, LANES), jnp.float32))
     square_sum = jnp.sum(squares)
 
-    def expand(block, tile):
+    def expand(block, side, tile):
         lanes = lanes_of(tile)
         places = piece_lanes(tile)
         params = slots_ref[tile]
@@ -245,7 +276,7 @@
                 high, low = split(value)
                 start = part * XBLOCK + group * FINE
                 for where, piece in zip(places, (high, high, low)):
-                    lhs[block % 2, start : start + FINE, where] = piece
+                    lhs[side, start : start + FINE, where] = piece
 
     def image_copy(owner, sub):
         slot = lax.rem(owner - me_wa + blocks, blocks) - 1
@@ -277,18 +308,20 @@
 
     @pl.loop(0, tiles)
     def _(tile):
-        expand(0, tile)
+        expand(0, 0, tile)
 
     parts = blocks // 2
-    for block in range(block_total):
+    order = [first + part * subs for first in range(subs) for part in range(block_total // subs)]
+    for turn, block in enumerate(order):
+        following = order[turn + 1] if turn + 1 < block_total else None
 
         @pl.loop(0, tiles // 2)
         def _(chunk):
             wide = pl.ds(pl.multiple_of(chunk * (PIECES * CHUNK), LANES), PIECES * CHUNK)
-            product = dot_nt(lhs[block % 2, :, wide], rhs[:, wide])
-            if block + 1 < block_total:
-                expand(block + 1, chunk * 2)
-                expand(block + 1, chunk * 2 + 1)
+            product = dot_nt(lhs[turn % 2, :, wide], rhs[:, wide])
+            if following is not None:
+                expand(following, (turn + 1) % 2, chunk * 2)
+                expand(following, (turn + 1) % 2, chunk * 2 + 1)
             acc[...] = jnp.where(chunk == 0, 0.0, acc[...]) + product
 
         x_row = block * XBLOCK + lax.broadcasted_iota(jnp.int32, (XBLOCK, 1), 0)
@@ -389,7 +422,7 @@
     half = GRID // 2
     columns = 2 * layer_dev * pixels
     vmem = pl.BlockSpec(memory_space=pltpu.VMEM)
-    smem = pl.BlockSpec(memory_space=pltpu.SMEM)
+    anywhere = pl.BlockSpec(memory_space=pltpu.HBM)
     f32, bf16 = jnp.float32, jnp.bfloat16
     shapes = [
         ((own_tiles, 8, LANES), f32),
@@ -423,18 +456,32 @@
     return pl.pallas_call(
         functools.partial(kernel, layer_dev, pixels, blocks, peers),
         out_shape=jax.ShapeDtypeStruct((chunk_rows, pixels), f32),
-        in_specs=[smem, smem] + [vmem] * 6,
+        in_specs=[anywhere] * 8,
         out_specs=vmem,
-        scratch_shapes=[pltpu.VMEM(shape, kind) for shape, kind in shapes]
+        scratch_shapes=[pltpu.SMEM(layer_depth.shape, f32)]
+        + [
+            pltpu.VMEM(value.shape, value.dtype)
+            for value in (
+                tile_counts,
+                kernel_table.T,
+                visibilities,
+                weights,
+                cell_index,
+                kernel_index,
+                layer_index,
+            )
+        ]
+        + [pltpu.SemaphoreType.DMA((8,))]
+        + [pltpu.VMEM(shape, kind) for shape, kind in shapes]
         + [pltpu.SemaphoreType.DMA(shape) for shape in semaphores],
         compiler_params=pltpu.CompilerParams(
-            collective_id=0, has_side_effects=True, vmem_limit_bytes=48 * 1024 * 1024
+            collective_id=0, has_side_effects=True, vmem_limit_bytes=67043328
         ),
         name="dirty_image",
     )(
         layer_depth,
         tile_counts,
-        kernel_table,
+        kernel_table.T,
         visibilities,
         weights,
         cell_index,

time: 35.3 us -> 35.6 us (level)
    unnamed x16 -> x1, local copies, waits for them, and re-layouts: 1.52 us -> 1.57 us
where the time goes in v2:
time: 35.6 us; the launch traced here: 35.4 us
  Pallas kernels  33.9 us (95%)
  local copies, waits for them, and re-layouts  1.57 us (4%)
    pallas_call x1, Pallas kernels, body(): pl.pallas_call(functools.partial(kernel, layer_dev, pixels, blocks, peers...  33.9 us
    unnamed x1, local copies, waits for them, and re-layouts  1.57 us

profile of v2, /device:TPU:0, one launch (start us, length us, event | category | flops | bytes accessed | tf_op | source)
XLA Modules:
  0.0 35.4 jit_solution(16707096695259578839)
XLA Ops:
  0.0 33.9 %dirty_image.1 = f32[256,128]{1,0:T(8,128)} custom-call(f32[2]{0:T(128)} %depth_hbm.1, s32[1,2]{1,0:T(1,128)} %counts_hbm.1, f32[8,16]{1,0:T(8,128)} %bitcast.1, f32[1,2,2,128]{3,2,1,0:T(2,128)} %vis_hbm.1, f32[1,2,128]{2,1,0:T(2,128)} %weight_hbm.1, s32[1,2,128]{2,1,0:T(2,128)} %cell_hbm.1, s32[1,2,128]{2,1,0:T(2,128)} %index_hbm.1, s32[1,2,128]{2,1,0:T(2,128)} %layer_hbm.1), custom_call_target="tpu_custom_call" | custom-call | tf_op jit(solution)/shard_map/dirty_image/pallas_call | solution.py:456
  33.9 1.6 %copy.10 = f32[256,128]{1,0:T(8,128)} copy(f32[256,128]{1,0:T(8,128)} %dirty_image.1) | data formatting | bytes 262144

commit v3 on v2

--- a/solution.py
+++ b/solution.py
@@ -111,7 +111,10 @@
     coarse_re,
     coarse_im,
     rhs,
-    lhs,
+    lhs_even,
+    lhs_odd,
+    rhs_even,
+    rhs_odd,
     acc,
     image,
     tail,
@@ -130,6 +133,7 @@
     tiles = peers * own_tiles
     block_total = half // XBLOCK
     subs = chunk_rows // XBLOCK
+    block_groups = XBLOCK // FINE
     me_bl, me_wa = lax.axis_index("bl"), lax.axis_index("wa")
     loads = [
         pltpu.make_async_copy(source, target, load_sem.at[place])
@@ -212,16 +216,25 @@
             pl.ds(pl.multiple_of(base + piece * CHUNK, LANES), LANES) for piece in range(PIECES)
         ]
 
-    def prepare(tile, square):
+    def stage_lanes(part_of_chunk):
+        starts = [piece * CHUNK + part_of_chunk * LANES for piece in range(PIECES)]
+        return [slice(start, start + LANES) for start in starts]
+
+    def prepare(tile, stage, part_of_chunk):
         lanes = lanes_of(tile)
         places = piece_lanes(tile)
+        staged = stage_lanes(part_of_chunk)
         params = slots_ref[tile]
-        vis_real, vis_imag, weight = params[0:1], params[1:2], params[2:3]
+        vis_real, vis_imag = params[0:1], params[1:2]
         row, col = params[3:4] * (1.0 / GRID), params[4:5] * (1.0 / GRID)
         col_kernel = params[6:7].astype(jnp.int32)
         layer = params[7:8]
         fine_re[:, lanes], fine_im[:, lanes] = turn_cos_sin(row * fine_x)
-        coarse_re[:, lanes], coarse_im[:, lanes] = turn_cos_sin(row * coarse_x)
+        cx_re, cx_im = turn_cos_sin(row * coarse_x)
+        for block in range(block_total):
+            lines = slice(block * block_groups, (block + 1) * block_groups)
+            coarse_re[block, :, lanes] = cx_re[lines]
+            coarse_im[block, :, lanes] = cx_im[lines]
         cf_re, cf_im = turn_cos_sin(col * fine_x)
         cc_re, cc_im = turn_cos_sin(col * pixel_y)
         cv_re = cc_re * vis_real - cc_im * vis_imag
@@ -243,40 +256,39 @@
                 for place, value in enumerate((real, imag)):
                     high, low = split(value * masks[item])
                     start = (item * 2 + place) * pixels + group * FINE
-                    for where, piece in zip(places, (high, low, high)):
+                    for where, near, piece in zip(places, staged, (high, low, high)):
                         rhs[start : start + FINE, where] = piece
-        return square + weight * weight
-
-    squares = lax.fori_loop(0, tiles, prepare, jnp.zeros((1, LANES), jnp.float32))
-    square_sum = jnp.sum(squares)
-
-    def expand(block, side, tile):
+                        stage[start : start + FINE, near] = piece
+
+    square_sum = jnp.sum(slots_ref[:, 2:3, :] * slots_ref[:, 2:3, :])
+
+    def expand(block, side, tile, part_of_chunk):
         lanes = lanes_of(tile)
-        places = piece_lanes(tile)
+        places = stage_lanes(part_of_chunk)
         params = slots_ref[tile]
         index = jnp.broadcast_to(params[5:6].astype(jnp.int32), (FINE, LANES))
         f_re, f_im = fine_re[:, lanes], fine_im[:, lanes]
+        c_re, c_im = coarse_re[block, :, lanes], coarse_im[block, :, lanes]
         for group in range(XBLOCK // FINE):
             place = block * (XBLOCK // FINE) + group
-            rows = slice(place * FINE, (place + 1) * FINE)
+            rows = pl.ds(pl.multiple_of(place * FINE, FINE), FINE)
             k_re = jnp.take_along_axis(u_re[rows, :], index, axis=1, mode="promise_in_bounds")
             k_im = jnp.take_along_axis(u_im[rows, :], index, axis=1, mode="promise_in_bounds")
-            g_re = coarse_re[place : place + 1, lanes]
-            g_im = coarse_im[place : place + 1, lanes]
+            g_re, g_im = c_re[group : group + 1], c_im[group : group + 1]
             e_re = f_re * g_re - f_im * g_im
             e_im = f_re * g_im + f_im * g_re
             real = e_re * k_re - e_im * k_im
             imag = e_re * k_im + e_im * k_re
-            if place == 0:
+            if group == 0:
                 odd = params[3:4].astype(jnp.int32) % 2
                 sign = (1 - 2 * odd).astype(jnp.float32)
                 first_row = lax.broadcasted_iota(jnp.int32, (FINE, LANES), 0) == 0
-                imag = imag * jnp.where(first_row, sign, 1.0)
+                imag = imag * jnp.where(first_row & (block == 0), sign, 1.0)
             for part, value in enumerate((real, imag)):
                 high, low = split(value)
                 start = part * XBLOCK + group * FINE
                 for where, piece in zip(places, (high, high, low)):
-                    lhs[side, start : start + FINE, where] = piece
+                    side[start : start + FINE, where] = piece
 
     def image_copy(owner, sub):
         slot = lax.rem(owner - me_wa + blocks, blocks) - 1
@@ -306,23 +318,33 @@
     top_depth = jnp.sqrt(1.0 - y_coord * y_coord) - 1.0
     tail[...] = jnp.full_like(tail, square_sum)
 
-    @pl.loop(0, tiles)
-    def _(tile):
-        expand(0, 0, tile)
+    chunks = tiles // 2
+    lhs_sides, rhs_sides = (lhs_even, lhs_odd), (rhs_even, rhs_odd)
+    for part_of_chunk in range(2):
+        prepare(part_of_chunk, rhs_even, part_of_chunk)
+        expand(0, lhs_even, part_of_chunk, part_of_chunk)
 
     parts = blocks // 2
     order = [first + part * subs for first in range(subs) for part in range(block_total // subs)]
     for turn, block in enumerate(order):
-        following = order[turn + 1] if turn + 1 < block_total else None
-
-        @pl.loop(0, tiles // 2)
-        def _(chunk):
-            wide = pl.ds(pl.multiple_of(chunk * (PIECES * CHUNK), LANES), PIECES * CHUNK)
-            product = dot_nt(lhs[turn % 2, :, wide], rhs[:, wide])
-            if following is not None:
-                expand(following, (turn + 1) % 2, chunk * 2)
-                expand(following, (turn + 1) % 2, chunk * 2 + 1)
-            acc[...] = jnp.where(chunk == 0, 0.0, acc[...]) + product
+        following = order[turn + 1] if turn + 1 < block_total else block
+
+        @pl.loop(0, chunks // 2)
+        def _(couple):
+            total = jnp.where(couple == 0, 0.0, acc[...])
+            for parity in range(2):
+                chunk = couple * 2 + parity
+                wide = pl.ds(pl.multiple_of(chunk * (PIECES * CHUNK), LANES), PIECES * CHUNK)
+                right = rhs[:, wide] if turn else rhs_sides[parity][...]
+                total = total + dot_nt(lhs_sides[parity][...], right)
+                coming = lax.rem(chunk + 1, chunks)
+                coming_block = jnp.where(coming == 0, following, block)
+                for part_of_chunk in range(2):
+                    tile = coming * 2 + part_of_chunk
+                    if turn == 0:
+                        prepare(tile, rhs_sides[1 - parity], part_of_chunk)
+                    expand(coming_block, lhs_sides[1 - parity], tile, part_of_chunk)
+            acc[...] = total
 
         x_row = block * XBLOCK + lax.broadcasted_iota(jnp.int32, (XBLOCK, 1), 0)
         x_coord = (x_row - GRID // 2).astype(jnp.float32) * (field_of_view / GRID)
@@ -434,10 +456,13 @@
         ((pixels, LANES), f32),
         ((FINE, count), f32),
         ((FINE, count), f32),
-        ((half // FINE, count), f32),
-        ((half // FINE, count), f32),
+        ((half // XBLOCK, XBLOCK // FINE, count), f32),
+        ((half // XBLOCK, XBLOCK // FINE, count), f32),
         ((columns, PIECES * count), bf16),
-        ((2, 2 * XBLOCK, PIECES * count), bf16),
+        ((2 * XBLOCK, PIECES * CHUNK), bf16),
+        ((2 * XBLOCK, PIECES * CHUNK), bf16),
+        ((columns, PIECES * CHUNK), bf16),
+        ((columns, PIECES * CHUNK), bf16),
         ((2 * XBLOCK, columns), f32),
         ((blocks, chunk_rows, pixels), f32),
         ((blocks, 8, pixels), f32),
@@ -475,7 +500,7 @@
         + [pltpu.VMEM(shape, kind) for shape, kind in shapes]
         + [pltpu.SemaphoreType.DMA(shape) for shape in semaphores],
         compiler_params=pltpu.CompilerParams(
-            collective_id=0, has_side_effects=True, vmem_limit_bytes=67043328
+            collective_id=0, has_side_effects=True, vmem_limit_bytes=48 * 1024 * 1024
         ),
         name="dirty_image",
     )(

time: 35.6 us -> 33.8 us (0.949)
  Pallas kernels: 33.9 us -> 28.1 us
  local copies, waits for them, and re-layouts: 1.57 us -> 5.41 us
    pallas_call x1, Pallas kernels: 33.9 us -> 28.1 us  [body(): pl.pallas_call(functools.partial(kernel, layer_dev, pixels, blocks, peers...]
    unnamed x1 -> x17, local copies, waits for them, and re-layouts: 1.57 us -> 5.41 us
where the time goes in v3:
time: 33.8 us; the launch traced here: 33.5 us
  Pallas kernels  28.1 us (83%)
  local copies, waits for them, and re-layouts  5.41 us (16%)
    pallas_call x1, Pallas kernels, body(): pl.pallas_call(functools.partial(kernel, layer_dev, pixels, blocks, peers...  28.1 us
    unnamed x17, local copies, waits for them, and re-layouts  5.41 us

profile of v3, /device:TPU:0, one launch (start us, length us, event | category | flops | bytes accessed | tf_op | source)
XLA Modules:
  0.0 33.5 jit_solution(17522013476615572557)
XLA Ops:
  0.0 0.0 copy-start.6
  0.0 0.0 copy-start.2
  0.0 0.7 %copy-done.6 = f32[2]{0:T(128)S(1)} copy-done((f32[2]{0:T(128)S(1)}, f32[2]{0:T(128)}, u32[]{:S(2)}) %copy-start.6) | copy-done | bytes 32
  0.7 0.0 copy-done.2
  0.7 0.0 copy-start
  0.7 0.7 %copy-done = f32[16,8]{0,1:T(8,128)S(1)} copy-done((f32[16,8]{0,1:T(8,128)S(1)}, f32[16,8]{0,1:T(8,128)}, u32[]{:S(2)}) %copy-start) | copy-done | bytes 536
  1.4 0.0 copy-start.1
  1.4 0.7 %copy-done.1 = f32[1,2,2,128]{3,2,1,0:T(2,128)S(1)} copy-done((f32[1,2,2,128]{3,2,1,0:T(2,128)S(1)}, f32[1,2,2,128]{3,2,1,0:T(2,128)}, u32[]{:S(2)}) %copy-start.1) | copy-done | bytes 2072
  2.1 0.0 copy-start.3
  2.1 0.7 %copy-done.3 = s32[1,2,128]{2,1,0:T(2,128)S(1)} copy-done((s32[1,2,128]{2,1,0:T(2,128)S(1)}, s32[1,2,128]{2,1,0:T(2,128)}, u32[]{:S(2)}) %copy-start.3) | copy-done | bytes 1048
  2.7 0.0 copy-start.4
  2.7 0.7 %copy-done.4 = s32[1,2,128]{2,1,0:T(2,128)S(1)} copy-done((s32[1,2,128]{2,1,0:T(2,128)S(1)}, s32[1,2,128]{2,1,0:T(2,128)}, u32[]{:S(2)}) %copy-start.4) | copy-done | bytes 1048
  3.4 0.0 copy-start.5
  3.4 0.7 %copy-done.5 = s32[1,2,128]{2,1,0:T(2,128)S(1)} copy-done((s32[1,2,128]{2,1,0:T(2,128)S(1)}, s32[1,2,128]{2,1,0:T(2,128)}, u32[]{:S(2)}) %copy-start.5) | copy-done | bytes 1048
  4.1 0.0 copy-start.7
  4.1 0.7 %copy-done.7 = s32[1,2]{1,0:T(1,128)S(1)} copy-done((s32[1,2]{1,0:T(1,128)S(1)}, s32[1,2]{1,0:T(1,128)}, u32[]{:S(2)}) %copy-start.7) | copy-done | bytes 32
  4.8 28.1 %dirty_image.1 = f32[256,128]{1,0:T(8,128)S(1)} custom-call(f32[2]{0:T(128)S(1)} %copy-done.6, s32[1,2]{1,0:T(1,128)S(1)} %copy-done.7, f32[8,16]{1,0:T(8,128)S(1)} %bitcast.1, f32[1,2,2,128]{3,2,1,0:T(2,128)S(1)} %copy-done.1, f32[1,2,128]{2,1,0:T(2,128)S(1)} %copy-done.2, s32[1,2,128]{2,1,0:T(2,128)S(1)} %copy-done.3, s32[1,2,128]{2,1,0:T(2,128)S(1)} %copy-done.4, ...), custom_call_target="tpu_custom_call" | custom-call | tf_op jit(solution)/shard_map/dirty_image/pallas_call | solution.py:481
  32.9 0.7 %copy.10 = f32[256,128]{1,0:T(8,128)} copy(f32[256,128]{1,0:T(8,128)S(1)} %dirty_image.1) | data formatting | bytes 262144
Async XLA Ops:
  0.0 0.7 %copy-start.6 = (f32[2]{0:T(128)S(1)}, f32[2]{0:T(128)}, u32[]{:S(2)}) copy-start(f32[2]{0:T(128)} %depth_hbm.1) | copy-start | bytes 28
  0.0 0.7 %copy-start.2 = (f32[1,2,128]{2,1,0:T(2,128)S(1)}, f32[1,2,128]{2,1,0:T(2,128)}, u32[]{:S(2)}) copy-start(f32[1,2,128]{2,1,0:T(2,128)} %weight_hbm.1) | copy-start | bytes 3076
  0.7 0.7 %copy-start = (f32[16,8]{0,1:T(8,128)S(1)}, f32[16,8]{0,1:T(8,128)}, u32[]{:S(2)}) copy-start(f32[16,8]{0,1:T(8,128)} %param.14) | copy-start | bytes 1540
  1.4 0.7 %copy-start.1 = (f32[1,2,2,128]{3,2,1,0:T(2,128)S(1)}, f32[1,2,2,128]{3,2,1,0:T(2,128)}, u32[]{:S(2)}) copy-start(f32[1,2,2,128]{3,2,1,0:T(2,128)} %vis_hbm.1) | copy-start | bytes 6148
  2.1 0.7 %copy-start.3 = (s32[1,2,128]{2,1,0:T(2,128)S(1)}, s32[1,2,128]{2,1,0:T(2,128)}, u32[]{:S(2)}) copy-start(s32[1,2,128]{2,1,0:T(2,128)} %cell_hbm.1) | copy-start | bytes 3076
  2.7 0.7 %copy-start.4 = (s32[1,2,128]{2,1,0:T(2,128)S(1)}, s32[1,2,128]{2,1,0:T(2,128)}, u32[]{:S(2)}) copy-start(s32[1,2,128]{2,1,0:T(2,128)} %index_hbm.1) | copy-start | bytes 3076
  3.4 0.7 %copy-start.5 = (s32[1,2,128]{2,1,0:T(2,128)S(1)}, s32[1,2,128]{2,1,0:T(2,128)}, u32[]{:S(2)}) copy-start(s32[1,2,128]{2,1,0:T(2,128)} %layer_hbm.1) | copy-start | bytes 3076
  4.1 0.7 %copy-start.7 = (s32[1,2]{1,0:T(1,128)S(1)}, s32[1,2]{1,0:T(1,128)}, u32[]{:S(2)}) copy-start(s32[1,2]{1,0:T(1,128)} %counts_hbm.1) | copy-start | bytes 28

commit v4 on v3

--- a/solution.py
+++ b/solution.py
@@ -21,8 +21,8 @@
 MESH = pl.DeviceIdType.MESH
 
 TWO_PI = 2.0 * math.pi
-SIN_TERMS = [(-1) ** k * TWO_PI ** (2 * k + 1) / math.factorial(2 * k + 1) for k in range(9)]
-COS_TERMS = [(-1) ** k * TWO_PI ** (2 * k) / math.factorial(2 * k) for k in range(10)]
+SIN_TERMS = [(-1) ** k * TWO_PI ** (2 * k + 1) / math.factorial(2 * k + 1) for k in range(8)]
+COS_TERMS = [(-1) ** k * TWO_PI ** (2 * k) / math.factorial(2 * k) for k in range(9)]
 
 
 def horner(square, terms):
@@ -62,13 +62,9 @@
 
     def product(part):
         high, low = split(part)
-        return dot_nn(high, table_high) + dot_nn(high, table_low) + dot_nn(low, table_high)
+        return dot_nt(high, table_high) + dot_nt(high, table_low) + dot_nt(low, table_high)
 
     return product(cos_part), product(sin_part)
-
-
-def dot_nn(a, b):
-    return jnp.dot(a, b, preferred_element_type=jnp.float32)
 
 
 def start_all(copies):
@@ -81,15 +77,6 @@
     pixels,
     blocks,
     peers,
-    depth_hbm,
-    counts_hbm,
-    table_hbm,
-    vis_hbm,
-    weight_hbm,
-    cell_hbm,
-    index_hbm,
-    layer_hbm,
-    out_ref,
     depth_ref,
     counts_ref,
     table_ref,
@@ -98,7 +85,7 @@
     cell_ref,
     index_ref,
     layer_ref,
-    load_sem,
+    out_ref,
     own,
     slots_ref,
     table_pad,
@@ -135,34 +122,16 @@
     subs = chunk_rows // XBLOCK
     block_groups = XBLOCK // FINE
     me_bl, me_wa = lax.axis_index("bl"), lax.axis_index("wa")
-    loads = [
-        pltpu.make_async_copy(source, target, load_sem.at[place])
-        for place, (source, target) in enumerate(
-            (
-                (counts_hbm, counts_ref),
-                (vis_hbm, vis_ref),
-                (weight_hbm, weight_ref),
-                (cell_hbm, cell_ref),
-                (index_hbm, index_ref),
-                (layer_hbm, layer_ref),
-                (table_hbm, table_ref),
-                (depth_hbm, depth_ref),
-            )
-        )
-    ]
-    start_all(loads)
     barrier = pltpu.get_barrier_semaphore()
     for axis, me, count in (("bl", me_bl, peers), ("wa", me_wa, blocks)):
         for step in range(1, count):
             pl.semaphore_signal(
                 barrier, inc=1, device_id={axis: lax.rem(me + step, count)}, device_id_type=MESH
             )
-    for load in loads:
-        load.wait()
     position = lax.broadcasted_iota(jnp.int32, (1, LANES), 1)
     for tile in range(own_tiles):
         line = slice(tile, tile + 1)
-        weight = jnp.where(position < counts_ref[0:1, tile : tile + 1], weight_ref[0, line], 0.0)
+        weight = jnp.where(position < counts_ref[0, tile], weight_ref[0, line], 0.0)
         cell, index = cell_ref[0, line], index_ref[0, line]
         values = [
             vis_ref[0, tile, 0:1] * weight,
@@ -193,7 +162,7 @@
 
     first_pixel = me_bl * pixels
     table_pad[...] = jnp.zeros_like(table_pad)
-    table_pad[0:SUPPORT, 0:OVERSAMPLE] = table_ref[...]
+    table_pad[0:OVERSAMPLE, 0:SUPPORT] = table_ref[...]
     table = table_pad[...]
     u_re[...], u_im[...] = factor_table(0, half, table, True)
     v_re[...], v_im[...] = factor_table(first_pixel, pixels, table, False)
@@ -444,7 +413,7 @@
     half = GRID // 2
     columns = 2 * layer_dev * pixels
     vmem = pl.BlockSpec(memory_space=pltpu.VMEM)
-    anywhere = pl.BlockSpec(memory_space=pltpu.HBM)
+    smem = pl.BlockSpec(memory_space=pltpu.SMEM)
     f32, bf16 = jnp.float32, jnp.bfloat16
     shapes = [
         ((own_tiles, 8, LANES), f32),
@@ -481,23 +450,9 @@
     return pl.pallas_call(
         functools.partial(kernel, layer_dev, pixels, blocks, peers),
         out_shape=jax.ShapeDtypeStruct((chunk_rows, pixels), f32),
-        in_specs=[anywhere] * 8,
+        in_specs=[smem, smem] + [vmem] * 6,
         out_specs=vmem,
-        scratch_shapes=[pltpu.SMEM(layer_depth.shape, f32)]
-        + [
-            pltpu.VMEM(value.shape, value.dtype)
-            for value in (
-                tile_counts,
-                kernel_table.T,
-                visibilities,
-                weights,
-                cell_index,
-                kernel_index,
-                layer_index,
-            )
-        ]
-        + [pltpu.SemaphoreType.DMA((8,))]
-        + [pltpu.VMEM(shape, kind) for shape, kind in shapes]
+        scratch_shapes=[pltpu.VMEM(shape, kind) for shape, kind in shapes]
         + [pltpu.SemaphoreType.DMA(shape) for shape in semaphores],
         compiler_params=pltpu.CompilerParams(
             collective_id=0, has_side_effects=True, vmem_limit_bytes=48 * 1024 * 1024
@@ -506,7 +461,7 @@
     )(
         layer_depth,
         tile_counts,
-        kernel_table.T,
+        kernel_table,
         visibilities,
         weights,
         cell_index,

time: 33.8 us -> 30.1 us (0.89)
  local copies, waits for them, and re-layouts: 5.41 us -> 1.52 us
    unnamed x17 -> x16, local copies, waits for them, and re-layouts: 5.41 us -> 1.52 us
where the time goes in v4:
time: 30.1 us; the launch traced here: 30 us
  Pallas kernels  28.4 us (94%)
  local copies, waits for them, and re-layouts  1.52 us (5%)
    pallas_call x1, Pallas kernels, body(): pl.pallas_call(functools.partial(kernel, layer_dev, pixels, blocks, peers...  28.4 us
    unnamed x16, local copies, waits for them, and re-layouts  1.52 us

profile of v4, /device:TPU:0, one launch (start us, length us, event | category | flops | bytes accessed | tf_op | source)
XLA Modules:
  0.0 30.0 jit_solution(14660889282193623453)
XLA Ops:
  0.0 0.0 copy-start.5
  0.0 0.0 copy-start.6
  0.0 0.0 copy-start.4
  0.0 0.0 copy-start.3
  0.0 0.0 copy-start.2
  0.0 0.0 copy-start.1
  0.0 0.0 copy-start
  0.0 0.8 %copy.9.table_ref = f32[16,8]{1,0:T(8,128)S(1)} copy(f32[16,8]{0,1:T(8,128)} %param.14) | data formatting | bytes 1024 | tf_op args[6]
  0.9 0.0 copy-done.5
  0.9 0.0 copy-done.6
  0.9 0.0 copy-done.4
  0.9 0.0 copy-done.3
  0.9 0.0 copy-done.2
  0.9 0.0 copy-done.1
  0.9 0.0 copy-done
  0.9 28.4 %dirty_image.1 = f32[256,128]{1,0:T(8,128)S(1)} custom-call(f32[2]{0:T(128)S(1)} %copy-done.5, s32[1,2]{1,0:T(1,128)S(1)} %copy-done.6, f32[16,8]{1,0:T(8,128)S(1)} %copy.9.table_ref, f32[1,2,2,128]{3,2,1,0:T(2,128)S(1)} %copy-done, f32[1,2,128]{2,1,0:T(2,128)S(1)} %copy-done.1, s32[1,2,128]{2,1,0:T(2,128)S(1)} %copy-done.2, s32[1,2,128]{2,1,0:T(2,128)S(1)} %copy-done.3, ...), custom_call_target="tpu_custom_call" | custom-call | tf_op jit(solution)/shard_map/dirty_image/pallas_call | solution.py:450
  29.3 0.7 %copy.11 = f32[256,128]{1,0:T(8,128)} copy(f32[256,128]{1,0:T(8,128)S(1)} %dirty_image.1) | data formatting | bytes 262144
Async XLA Ops:
  0.0 0.9 %copy-start.5 = (f32[2]{0:T(128)S(1)}, f32[2]{0:T(128)}, u32[]{:S(2)}) copy-start(f32[2]{0:T(128)} %depth_ref.1) | copy-start | bytes 28
  0.0 0.9 %copy-start.6 = (s32[1,2]{1,0:T(1,128)S(1)}, s32[1,2]{1,0:T(1,128)}, u32[]{:S(2)}) copy-start(s32[1,2]{1,0:T(1,128)} %counts_ref.1) | copy-start | bytes 28
  0.0 0.9 %copy-start.4 = (s32[1,2,128]{2,1,0:T(2,128)S(1)}, s32[1,2,128]{2,1,0:T(2,128)}, u32[]{:S(2)}) copy-start(s32[1,2,128]{2,1,0:T(2,128)} %layer_ref.1) | copy-start | bytes 3076
  0.0 0.9 %copy-start.3 = (s32[1,2,128]{2,1,0:T(2,128)S(1)}, s32[1,2,128]{2,1,0:T(2,128)}, u32[]{:S(2)}) copy-start(s32[1,2,128]{2,1,0:T(2,128)} %index_ref.1) | copy-start | bytes 3076
  0.0 0.9 %copy-start.2 = (s32[1,2,128]{2,1,0:T(2,128)S(1)}, s32[1,2,128]{2,1,0:T(2,128)}, u32[]{:S(2)}) copy-start(s32[1,2,128]{2,1,0:T(2,128)} %cell_ref.1) | copy-start | bytes 3076
  0.0 0.9 %copy-start.1 = (f32[1,2,128]{2,1,0:T(2,128)S(1)}, f32[1,2,128]{2,1,0:T(2,128)}, u32[]{:S(2)}) copy-start(f32[1,2,128]{2,1,0:T(2,128)} %weight_ref.1) | copy-start | bytes 3076
  0.0 0.9 %copy-start = (f32[1,2,2,128]{3,2,1,0:T(2,128)S(1)}, f32[1,2,2,128]{3,2,1,0:T(2,128)}, u32[]{:S(2)}) copy-start(f32[1,2,2,128]{3,2,1,0:T(2,128)} %vis_ref.1) | copy-start | bytes 6148

commit v5 on v4

--- a/solution.py
+++ b/solution.py
@@ -89,6 +89,8 @@
     own,
     slots_ref,
     table_pad,
+    phase_cos,
+    phase_sin,
     u_re,
     u_im,
     v_re,
@@ -173,6 +175,18 @@
     pixel_y = (
         first_pixel + lax.broadcasted_iota(jnp.int32, (pixels // FINE, LANES), 0) * FINE
     ).astype(jnp.float32)
+    y_pixel = first_pixel + lax.broadcasted_iota(jnp.int32, (1, pixels), 1)
+    y_coord = (y_pixel - GRID // 2).astype(jnp.float32) * (field_of_view / GRID)
+    top_depth = jnp.sqrt(1.0 - y_coord * y_coord) - 1.0
+    for block in range(block_total):
+        x_row = block * XBLOCK + lax.broadcasted_iota(jnp.int32, (XBLOCK, 1), 0)
+        x_coord = (x_row - GRID // 2).astype(jnp.float32) * (field_of_view / GRID)
+        depth = jnp.sqrt(1.0 - x_coord * x_coord - y_coord * y_coord) - 1.0
+        lines = slice(block * XBLOCK, (block + 1) * XBLOCK)
+        for item in range(layer_dev):
+            cos_part, sin_part = turn_cos_sin(depth_ref[item] * depth)
+            phase_cos[item, lines, :] = cos_part
+            phase_sin[item, lines, :] = sin_part
     for copy in slot_copies:
         copy.wait()
 
@@ -282,9 +296,6 @@
             device_id_type=MESH,
         )
 
-    y_pixel = first_pixel + lax.broadcasted_iota(jnp.int32, (1, pixels), 1)
-    y_coord = (y_pixel - GRID // 2).astype(jnp.float32) * (field_of_view / GRID)
-    top_depth = jnp.sqrt(1.0 - y_coord * y_coord) - 1.0
     tail[...] = jnp.full_like(tail, square_sum)
 
     chunks = tiles // 2
@@ -316,8 +327,7 @@
             acc[...] = total
 
         x_row = block * XBLOCK + lax.broadcasted_iota(jnp.int32, (XBLOCK, 1), 0)
-        x_coord = (x_row - GRID // 2).astype(jnp.float32) * (field_of_view / GRID)
-        depth = jnp.sqrt(1.0 - x_coord * x_coord - y_coord * y_coord) - 1.0
+        lines = slice(block * XBLOCK, (block + 1) * XBLOCK)
         above = jnp.zeros((XBLOCK, pixels), jnp.float32)
         below = jnp.zeros((XBLOCK, pixels), jnp.float32)
         for item in range(layer_dev):
@@ -326,7 +336,7 @@
             p_ad = acc[:XBLOCK, first + pixels : first + 2 * pixels]
             p_bc = acc[XBLOCK:, first : first + pixels]
             p_bd = acc[XBLOCK:, first + pixels : first + 2 * pixels]
-            cos_part, sin_part = turn_cos_sin(depth_ref[item] * depth)
+            cos_part, sin_part = phase_cos[item, lines, :], phase_sin[item, lines, :]
             if block == 0:
                 top = x_row == 0
                 top_cos, top_sin = turn_cos_sin(depth_ref[item] * top_depth)
@@ -419,6 +429,8 @@
         ((own_tiles, 8, LANES), f32),
         ((tiles, 8, LANES), f32),
         ((LANES, LANES), f32),
+        ((layer_dev, half, pixels), f32),
+        ((layer_dev, half, pixels), f32),
         ((half, LANES), f32),
         ((half, LANES), f32),
         ((pixels, LANES), f32),

time: 30.1 us -> 29.9 us (level)
  no operation moved by 1% of the time
where the time goes in v5:
time: 29.9 us; the launch traced here: 29.8 us
  Pallas kernels  28.2 us (94%)
  local copies, waits for them, and re-layouts  1.52 us (5%)
    pallas_call x1, Pallas kernels, body(): pl.pallas_call(functools.partial(kernel, layer_dev, pixels, blocks, peers...  28.2 us
    unnamed x16, local copies, waits for them, and re-layouts  1.52 us

profile of v5, /device:TPU:0, one launch (start us, length us, event | category | flops | bytes accessed | tf_op | source)
XLA Modules:
  0.0 29.8 jit_solution(8000537419960093183)
XLA Ops:
  0.0 0.0 copy-start.5
  0.0 0.0 copy-start.6
  0.0 0.0 copy-start.4
  0.0 0.0 copy-start.3
  0.0 0.0 copy-start.2
  0.0 0.0 copy-start.1
  0.0 0.0 copy-start
  0.0 0.8 %copy.9.table_ref = f32[16,8]{1,0:T(8,128)S(1)} copy(f32[16,8]{0,1:T(8,128)} %param.14) | data formatting | bytes 1024 | tf_op args[6]
  0.9 0.0 copy-done.5
  0.9 0.0 copy-done.6
  0.9 0.0 copy-done.4
  0.9 0.0 copy-done.3
  0.9 0.0 copy-done.2
  0.9 0.0 copy-done.1
  0.9 0.0 copy-done
  0.9 28.2 %dirty_image.1 = f32[256,128]{1,0:T(8,128)S(1)} custom-call(f32[2]{0:T(128)S(1)} %copy-done.5, s32[1,2]{1,0:T(1,128)S(1)} %copy-done.6, f32[16,8]{1,0:T(8,128)S(1)} %copy.9.table_ref, f32[1,2,2,128]{3,2,1,0:T(2,128)S(1)} %copy-done, f32[1,2,128]{2,1,0:T(2,128)S(1)} %copy-done.1, s32[1,2,128]{2,1,0:T(2,128)S(1)} %copy-done.2, s32[1,2,128]{2,1,0:T(2,128)S(1)} %copy-done.3, ...), custom_call_target="tpu_custom_call" | custom-call | tf_op jit(solution)/shard_map/dirty_image/pallas_call | solution.py:462
  29.1 0.7 %copy.11 = f32[256,128]{1,0:T(8,128)} copy(f32[256,128]{1,0:T(8,128)S(1)} %dirty_image.1) | data formatting | bytes 262144
Async XLA Ops:
  0.0 0.9 %copy-start.5 = (f32[2]{0:T(128)S(1)}, f32[2]{0:T(128)}, u32[]{:S(2)}) copy-start(f32[2]{0:T(128)} %depth_ref.1) | copy-start | bytes 28
  0.0 0.9 %copy-start.6 = (s32[1,2]{1,0:T(1,128)S(1)}, s32[1,2]{1,0:T(1,128)}, u32[]{:S(2)}) copy-start(s32[1,2]{1,0:T(1,128)} %counts_ref.1) | copy-start | bytes 28
  0.0 0.9 %copy-start.4 = (s32[1,2,128]{2,1,0:T(2,128)S(1)}, s32[1,2,128]{2,1,0:T(2,128)}, u32[]{:S(2)}) copy-start(s32[1,2,128]{2,1,0:T(2,128)} %layer_ref.1) | copy-start | bytes 3076
  0.0 0.9 %copy-start.3 = (s32[1,2,128]{2,1,0:T(2,128)S(1)}, s32[1,2,128]{2,1,0:T(2,128)}, u32[]{:S(2)}) copy-start(s32[1,2,128]{2,1,0:T(2,128)} %index_ref.1) | copy-start | bytes 3076
  0.0 0.9 %copy-start.2 = (s32[1,2,128]{2,1,0:T(2,128)S(1)}, s32[1,2,128]{2,1,0:T(2,128)}, u32[]{:S(2)}) copy-start(s32[1,2,128]{2,1,0:T(2,128)} %cell_ref.1) | copy-start | bytes 3076
  0.0 0.9 %copy-start.1 = (f32[1,2,128]{2,1,0:T(2,128)S(1)}, f32[1,2,128]{2,1,0:T(2,128)}, u32[]{:S(2)}) copy-start(f32[1,2,128]{2,1,0:T(2,128)} %weight_ref.1) | copy-start | bytes 3076
  0.0 0.9 %copy-start = (f32[1,2,2,128]{3,2,1,0:T(2,128)S(1)}, f32[1,2,2,128]{3,2,1,0:T(2,128)}, u32[]{:S(2)}) copy-start(f32[1,2,2,128]{3,2,1,0:T(2,128)} %vis_ref.1) | copy-start | bytes 6148
